TPU v7x, 32 devices: a whole 2x2x4 slice. The times are simulated.
32 devices in a mesh: grp: 8 (over z, y), mem: 4 (over x, core).
Axes of the slice: x: 2, y: 2, z: 4, core: 2. Of those that a mesh axis runs over, the one named last changes fastest.
Arguments:
- client_input: bfloat16 [8, 4, 128, 896], P('grp', 'mem'), may hold values from -6 to 6
- client_gain: float32 [4, 896], P('mem'), may hold values from 0.5 to 1.5
- w_query: bfloat16 [4, 896, 896], P('mem'), may hold values from -1.5 to 1.5
- w_keyval: bfloat16 [4, 896, 256], P('mem'), may hold values from -0.5 to 0.5
- w_out: bfloat16 [4, 896, 896], P('mem'), may hold values from -0.1875 to 0.1875
- server_gain: float32 [8, 896], P('grp'), may hold values from 0.5 to 1.5
- w_gate: bfloat16 [8, 896, 4864], P('grp', None, 'mem'), may hold values from -0.1875 to 0.1875
- w_up: bfloat16 [8, 896, 4864], P('grp', None, 'mem'), may hold values from -0.1875 to 0.1875
- w_down: bfloat16 [8, 4864, 896], P('grp', 'mem'), may hold values from -0.078125 to 0.078125
- out_grad: bfloat16 [8, 4, 128, 896], P('grp', 'mem'), may hold values from -6 to 6
- valid: int32 [8, 4], P('grp', 'mem'), may hold values from 64 to 128
Outputs:
- server_out: bfloat16 [8, 4, 128, 896], P('grp', 'mem')
- grad_query: bfloat16 [4, 896, 896], P('mem')
- grad_keyval: bfloat16 [4, 896, 256], P('mem')
- grad_out: bfloat16 [4, 896, 896], P('mem')
- grad_gate: bfloat16 [8, 896, 4864], P('grp', None, 'mem')
- grad_up: bfloat16 [8, 896, 4864], P('grp', None, 'mem')
- grad_down: bfloat16 [8, 4864, 896], P('grp', 'mem')
All inputs are finite; a program needn't handle non-finite values.
Results may differ from a plain program's by a relative error of at most 0.03.
Values may be sent and summed in bfloat16 or wider, within the bound.
A program may use at most 128 MiB of HBM per device.

v0:
```python
import jax
import jax.numpy as jnp
from jax import lax
from jax.experimental import pallas as pl
from jax.experimental.pallas import tpu as pltpu
from jax.sharding import PartitionSpec as P

KV_HEADS = 2
HEAD_DIM = 64


EPS = 1e-06
F32 = jnp.float32
BF16 = jnp.bfloat16
CONTRACT_LAST = (((1,), (1,)), ((), ()))
CONTRACT_FIRST = (((0,), (0,)), ((), ()))


def rms(h_float):
    return lax.rsqrt(jnp.mean(h_float * h_float, axis=-1, keepdims=True) + EPS)


def norm_back(h_float, inv_rms, gain_vec, upstream):
    scaled = upstream * gain_vec
    return inv_rms * scaled - h_float * inv_rms**3 * jnp.mean(
        scaled * h_float, axis=-1, keepdims=True
    )


def attention(queries, key_vals):
    length = queries.shape[0]
    half_cols = KV_HEADS * HEAD_DIM
    q_heads = queries.reshape(length, KV_HEADS, -1, HEAD_DIM)
    k_heads = key_vals[:, :half_cols].reshape(length, KV_HEADS, HEAD_DIM)
    v_heads = key_vals[:, half_cols:].reshape(length, KV_HEADS, HEAD_DIM)
    scores = jnp.einsum(
        "tgqd,sgd->gqts", q_heads, k_heads, preferred_element_type=F32
    ) * HEAD_DIM ** (-0.5)
    causal = jnp.arange(length)[:, None] >= jnp.arange(length)[None, :]
    scores = jnp.where(causal, scores, -1e30)
    highest = jnp.max(scores, axis=-1, keepdims=True)
    expo = jnp.exp(scores - highest)
    probs = (expo / jnp.sum(expo, axis=-1, keepdims=True)).astype(BF16)
    attended = jnp.einsum("gqts,sgd->tgqd", probs, v_heads, preferred_element_type=F32)
    return attended.astype(BF16).reshape(length, -1)


MESH = pl.DeviceIdType.MESH


class Gather:
    def __init__(self, axis, own, slots, sems):
        self.axis, self.own, self.slots, self.sems = axis, own, slots, sems
        self.n = lax.axis_size(axis)
        self.pairs = self.n // 2
        me = lax.axis_index(axis)
        self.right = {axis: lax.rem(me + 2, self.n)}
        self.partner = {axis: me + 1 - 2 * lax.rem(me, 2)}

    def source(self, step):
        return self.own if step == 0 else self.slots.at[2 * step]

    def ring_copy(self, step):
        ring_send, ring_recv = self.sems[0], self.sems[1]
        return pltpu.make_async_remote_copy(
            src_ref=self.source(step),
            dst_ref=self.slots.at[2 * step + 2],
            send_sem=ring_send.at[step],
            recv_sem=ring_recv.at[step],
            device_id=self.right,
            device_id_type=MESH,
        )

    def flip_copy(self, step):
        return pltpu.make_async_remote_copy(
            src_ref=self.source(step),
            dst_ref=self.slots.at[2 * step + 1],
            send_sem=self.sems[2].at[step],
            recv_sem=self.sems[3].at[step],
            device_id=self.partner,
            device_id_type=MESH,
        )

    def advance(self, step):
        if step > 0:
            self.ring_copy(step - 1).wait_recv()
        if step < self.pairs - 1:
            self.ring_copy(step).start()
        self.flip_copy(step).start()

    def take(self, step):
        self.flip_copy(step).wait_recv()

    def finish(self):
        for step in range(self.pairs):
            if step < self.pairs - 1:
                self.ring_copy(step).wait_send()
            self.flip_copy(step).wait_send()


def gather_sems(n):
    pairs = n // 2
    return [
        pltpu.SemaphoreType.DMA((max(pairs - 1, 1),)),
        pltpu.SemaphoreType.DMA((max(pairs - 1, 1),)),
        pltpu.SemaphoreType.DMA((pairs,)),
        pltpu.SemaphoreType.DMA((pairs,)),
    ]


def greet(axes):
    barrier = pltpu.get_barrier_semaphore()
    count = 0
    for axis in axes:
        n = lax.axis_size(axis)
        me = lax.axis_index(axis)
        pl.semaphore_signal(
            barrier, 1, device_id={axis: me + 1 - 2 * lax.rem(me, 2)}, device_id_type=MESH
        )
        for k in range(1, n // 2):
            pl.semaphore_signal(
                barrier, 1, device_id={axis: lax.rem(me + 2 * k, n)}, device_id_type=MESH
            )
        count += n // 2
    pl.semaphore_wait(barrier, count)


def send(src, dst, sems, index, device):
    return pltpu.make_async_remote_copy(
        src_ref=src,
        dst_ref=dst,
        send_sem=sems[0].at[index],
        recv_sem=sems[1].at[index],
        device_id=device,
        device_id_type=MESH,
    )


def server_kernel(
    cut_own, cot_own, attended_own, normed_own, gain, gate_hbm, up_hbm, down_hbm,
    server_out, cut_grad, attended_all, normed_all, rows_normed, rows_cot, hidden, d_gate, d_up,
    gate_w, up_w, down_w, cut_slots, served, served_in, home_in, home_out, sums, give, give_in,
    passing, pass_in, load_sem, cut_sems, cot_sems, attended_sems, normed_sems, swap_sems, part_sems,
    home_sems, pass_sems,
):
    members, groups = lax.axis_size("mem"), lax.axis_size("grp")
    pairs, group_pairs = members // 2, groups // 2
    length, width = cut_own.shape
    half = length // 2
    me = lax.axis_index("mem")
    odd = lax.rem(me, 2)
    partner = {"mem": me + 1 - 2 * odd}
    loads = []
    for i, (far, near) in enumerate(((down_hbm, down_w), (gate_hbm, gate_w), (up_hbm, up_w))):
        loads.append(pltpu.make_async_copy(far, near, load_sem.at[i]))
        loads[-1].start()
    greet(("grp", "mem"))
    cut = Gather("mem", cut_own, cut_slots, cut_sems)
    cot = Gather("mem", cot_own, rows_cot, cot_sems)
    early = [
        Gather("grp", normed_own, normed_all, normed_sems),
        Gather("grp", attended_own, attended_all, attended_sems),
    ]
    cut.advance(0)
    cot.advance(0)
    for chain in early:
        chain.advance(0)
    cut_slots[0] = cut_own[...]
    rows_cot[0] = cot_own[...]
    normed_all[0] = normed_own[...]
    attended_all[0] = attended_own[...]
    sums[...] = cot_own[...].astype(F32)
    swaps = []
    group_step = 1
    for p in range(pairs):
        if p > 0:
            cut.advance(p)
            cot.advance(p)
        cut.take(p)
        cot.take(p)
        span = pl.ds(2 * p, 2)
        h_float = cut_slots[span].reshape(2 * length, width).astype(F32)
        inv_rms = rms(h_float)
        normed = (h_float * inv_rms * gain[...]).astype(BF16)
        rows_normed[span] = normed.reshape(2, length, width)
        if p == 0:
            for load in loads:
                load.wait()
        d_hidden = lax.dot_general(
            rows_cot[span].reshape(2 * length, width), down_w[...], CONTRACT_LAST,
            preferred_element_type=F32,
        )
        gate_act = lax.dot_general(normed, gate_w[...], CONTRACT_LAST, preferred_element_type=F32)
        up_act = lax.dot_general(normed, up_w[...], CONTRACT_LAST, preferred_element_type=F32)
        sigma = jax.nn.sigmoid(gate_act)
        acted = gate_act * sigma
        hidden_now = (acted * up_act).astype(BF16)
        dg = (d_hidden * up_act * sigma * (1.0 + gate_act * (1.0 - sigma))).astype(BF16)
        du = (d_hidden * acted).astype(BF16)
        rows = pl.ds(2 * p * length, 2 * length)
        hidden[rows] = hidden_now
        d_gate[rows] = dg
        d_up[rows] = du
        d_normed = jnp.dot(dg, gate_w[...], preferred_element_type=F32)
        d_normed = d_normed + jnp.dot(du, up_w[...], preferred_element_type=F32)
        pushed = norm_back(h_float, inv_rms, gain[...], d_normed)
        sums[...] += pushed[:length] + pushed[length:]
        served[span] = (
            jnp.dot(hidden_now, down_w[...], preferred_element_type=F32)
            .astype(BF16)
            .reshape(2, length, width)
        )
        if group_step < group_pairs - 1:
            for chain in early:
                chain.advance(group_step)
            group_step += 1

    keep_rows = pl.ds(pl.multiple_of(odd * half, half), half)
    give_rows = pl.ds(pl.multiple_of((1 - odd) * half, half), half)
    give[...] = sums[give_rows].astype(BF16)
    handed = send(give, give_in, part_sems, 0, partner)
    handed.start()
    for p in range(pairs):
        swaps.append(send(served.at[2 * p + 1], served_in.at[p], swap_sems, p, partner))
        swaps[-1].start()
    handed.wait_recv()
    total = sums[keep_rows] + give_in[...].astype(F32)
    passing[...] = total.astype(BF16)
    passes = []
    for k in range(1, pairs):
        passes.append(
            send(passing, pass_in.at[k - 1], pass_sems, k - 1, {"mem": lax.rem(me + 2 * k, members)})
        )
        passes[-1].start()
    homes = []
    for p in range(pairs):
        swaps[p].wait_recv()
        mine = served[2 * p].astype(F32) + served_in[p].astype(F32)
        if p == 0:
            result = cut_own[...].astype(F32) + mine
            sums[...] = result
        else:
            home_out[p - 1] = mine.astype(BF16)
            homes.append(
                send(
                    home_out.at[p - 1], home_in.at[p - 1], home_sems, p - 1,
                    {"mem": lax.rem(me + members - 2 * p, members)},
                )
            )
            homes[-1].start()
    for k in range(1, pairs):
        passes[k - 1].wait_recv()
        total = total + pass_in[k - 1].astype(F32)
    cut_grad[keep_rows] = (total / members).astype(BF16)
    back = send(cut_grad.at[keep_rows], cut_grad.at[keep_rows], part_sems, 1, partner)
    back.start()
    result = sums[...]
    for p in range(1, pairs):
        homes[p - 1].wait_recv()
        result = result + home_in[p - 1].astype(F32)
    server_out[...] = result.astype(BF16)
    while group_step < group_pairs:
        for chain in early:
            chain.advance(group_step)
        group_step += 1
    for chain in early:
        for step in range(group_pairs):
            chain.take(step)
        chain.finish()
    cut.finish()
    cot.finish()
    back.wait_recv()
    for copy in [handed, back] + swaps + passes + homes:
        copy.wait_send()


def server_call(cut, cot, attended, normed, gain, gate_t, up_t, down):
    members, groups = lax.axis_size("mem"), lax.axis_size("grp")
    pairs = members // 2
    length, width = cut.shape
    units = down.shape[0]
    half = length // 2
    rows = members * length
    shape = jax.ShapeDtypeStruct
    vmem = pl.BlockSpec(memory_space=pltpu.VMEM)
    far = pl.BlockSpec(memory_space=pl.ANY)
    others = max(pairs - 1, 1)
    two = lambda count: [pltpu.SemaphoreType.DMA((count,))] * 2
    return pl.pallas_call(
        server_kernel,
        out_shape=[
            shape((length, width), BF16),
            shape((length, width), BF16),
            shape((groups, length, width), BF16),
            shape((groups, length, width), BF16),
            shape((members, length, width), BF16),
            shape((members, length, width), BF16),
            shape((rows, units), BF16),
            shape((rows, units), BF16),
            shape((rows, units), BF16),
        ],
        in_specs=[vmem] * 5 + [far] * 3,
        out_specs=[vmem] * 9,
        scratch_shapes=[
            pltpu.VMEM((units, width), BF16),
            pltpu.VMEM((units, width), BF16),
            pltpu.VMEM((units, width), BF16),
            pltpu.VMEM((members, length, width), BF16),
            pltpu.VMEM((members, length, width), BF16),
            pltpu.VMEM((pairs, length, width), BF16),
            pltpu.VMEM((others, length, width), BF16),
            pltpu.VMEM((others, length, width), BF16),
            pltpu.VMEM((length, width), F32),
            pltpu.VMEM((half, width), BF16),
            pltpu.VMEM((half, width), BF16),
            pltpu.VMEM((half, width), BF16),
            pltpu.VMEM((others, half, width), BF16),
            pltpu.SemaphoreType.DMA((3,)),
            gather_sems(members),
            gather_sems(members),
            gather_sems(groups),
            gather_sems(groups),
            two(pairs),
            two(2),
            two(others),
            two(others),
        ],
        compiler_params=pltpu.CompilerParams(
            collective_id=0, has_side_effects=True, vmem_limit_bytes=60 * 2**20
        ),
        name="server",
    )(cut, cot, attended, normed, gain, gate_t, up_t, down)


def grads_kernel(
    d_own, half_own, attended_all, normed_all, rows_normed, rows_cot, hidden, d_gate, d_up,
    grad_in, grad_out, grad_gate, grad_up, grad_down,
    d_slots, half_slots, half_in, acc, d_sems, half_sems, swap_sems,
):
    groups = lax.axis_size("grp")
    group_pairs = groups // 2
    half, width = half_own.shape
    length = 2 * half
    rows = rows_cot.shape[0] * length
    me = lax.axis_index("mem")
    odd = lax.rem(me, 2)
    partner = {"mem": me + 1 - 2 * odd}
    greet(("grp", "mem"))
    halves = Gather("grp", half_own, half_slots, half_sems)
    deltas = Gather("grp", d_own, d_slots, d_sems)
    chains = [halves, deltas]
    for chain in chains:
        chain.advance(0)
    half_slots[0] = half_own[...]
    d_slots[0] = d_own[...]
    acc_rows = acc.shape[0] // 2

    def weight_grad(left, right, out):
        right_now = right
        units = out.shape[0]
        out[...] = lax.dot_general(
            left[...], right_now, CONTRACT_FIRST, preferred_element_type=F32
        ).astype(BF16)

    cot = rows_cot[...].reshape(rows, width)
    normed = rows_normed[...].reshape(rows, width)
    jobs = [(hidden, cot, grad_down), (d_gate, normed, grad_gate), (d_up, normed, grad_up)]
    for step in range(1, group_pairs):
        if jobs:
            weight_grad(*jobs.pop(0))
        for chain in chains:
            chain.advance(step)
    while jobs:
        weight_grad(*jobs.pop(0))
    for step in range(group_pairs):
        halves.take(step)
    swap = send(half_slots, half_in, swap_sems, 0, partner)
    swap.start()
    ready = groups - 2
    for step in range(group_pairs - 1):
        deltas.take(step)
    scale = 1.0 / groups
    acc[...] = lax.dot_general(
        normed_all[pl.ds(0, ready)].reshape(ready * length, width),
        d_slots[pl.ds(0, ready)].reshape(ready * length, d_slots.shape[2]),
        CONTRACT_FIRST,
        preferred_element_type=F32,
    )
    swap.wait_recv()
    mine = half_slots[...]
    other = half_in[...]
    top = jnp.where(odd == 0, mine, other)
    bottom = jnp.where(odd == 0, other, mine)
    top_att = attended_all[:, pl.ds(0, half), :].reshape(groups * half, width)
    low_att = attended_all[:, pl.ds(half, half), :].reshape(groups * half, width)
    out = lax.dot_general(
        top_att, top.reshape(groups * half, width), CONTRACT_FIRST, preferred_element_type=F32
    )
    out = out + lax.dot_general(
        low_att, bottom.reshape(groups * half, width), CONTRACT_FIRST, preferred_element_type=F32
    )
    grad_out[...] = (out * scale).astype(BF16)
    deltas.take(group_pairs - 1)
    last = lax.dot_general(
        normed_all[pl.ds(ready, 2)].reshape(2 * length, width),
        d_slots[pl.ds(ready, 2)].reshape(2 * length, d_slots.shape[2]),
        CONTRACT_FIRST,
        preferred_element_type=F32,
    )
    grad_in[...] = ((acc[...] + last) * scale).astype(BF16)
    for chain in chains:
        chain.finish()
    swap.wait_send()


def grads_call(d_own, half_own, attended_all, normed_all, rows_normed, rows_cot, hidden, d_gate, d_up):
    groups = lax.axis_size("grp")
    half, width = half_own.shape
    length, wide = d_own.shape
    units = hidden.shape[1]
    shape = jax.ShapeDtypeStruct
    vmem = pl.BlockSpec(memory_space=pltpu.VMEM)
    return pl.pallas_call(
        grads_kernel,
        out_shape=[
            shape((width, wide), BF16),
            shape((width, width), BF16),
            shape((units, width), BF16),
            shape((units, width), BF16),
            shape((units, width), BF16),
        ],
        in_specs=[vmem] * 9,
        out_specs=[vmem] * 5,
        scratch_shapes=[
            pltpu.VMEM((groups, length, wide), BF16),
            pltpu.VMEM((groups, half, width), BF16),
            pltpu.VMEM((groups, half, width), BF16),
            pltpu.VMEM((width, wide), F32),
            gather_sems(groups),
            gather_sems(groups),
            [pltpu.SemaphoreType.DMA((1,))] * 2,
        ],
        compiler_params=pltpu.CompilerParams(
            collective_id=1, has_side_effects=True, vmem_limit_bytes=60 * 2**20
        ),
        name="grads",
    )(d_own, half_own, attended_all, normed_all, rows_normed, rows_cot, hidden, d_gate, d_up)


def on_device(
    client_input,
    client_gain,
    w_query,
    w_keyval,
    w_out,
    server_gain,
    w_gate,
    w_up,
    w_down,
    out_grad,
    valid,
):
    tokens_in = client_input[0, 0]
    output_w = w_out[0]
    length, width = tokens_in.shape
    half = length // 2
    odd = lax.axis_index("mem") % 2
    live = jnp.arange(length) < valid[0, 0]
    own_cot = jnp.where(live[:, None], out_grad[0, 0], jnp.zeros_like(out_grad[0, 0]))

    x_float = tokens_in.astype(F32)
    client_normed = (x_float * rms(x_float) * client_gain[0]).astype(BF16)
    queries = jnp.dot(client_normed, w_query[0], preferred_element_type=F32).astype(BF16)
    key_vals = jnp.dot(client_normed, w_keyval[0], preferred_element_type=F32).astype(BF16)
    attended, pull = jax.vjp(attention, queries, key_vals)
    mixed = jnp.dot(attended, output_w, preferred_element_type=F32)
    own_cut = (x_float + mixed).astype(BF16)

    (server_out, cut_grad, attended_all, normed_all, *rest) = server_call(
        own_cut, own_cot, attended, client_normed, server_gain, w_gate[0].T, w_up[0].T, w_down[0]
    )

    d_attended = lax.dot_general(
        cut_grad, output_w, CONTRACT_LAST, preferred_element_type=F32
    ).astype(BF16)
    d_queries, d_key_vals = pull(d_attended)
    half_grad = lax.dynamic_slice_in_dim(cut_grad, odd * half, half, 0)
    grad_in, grad_out, grad_gate, grad_up, grad_down = grads_call(
        jnp.concatenate([d_queries, d_key_vals], axis=1), half_grad, attended_all, normed_all, *rest
    )
    return (
        server_out[None, None],
        grad_in[None, :, : queries.shape[1]],
        grad_in[None, :, queries.shape[1] :],
        grad_out[None],
        grad_gate.T[None],
        grad_up.T[None],
        grad_down[None],
    )


def solution(mesh):
    in_specs = (
        P("grp", "mem", None, None),
        P("mem", None),
        P("mem", None, None),
        P("mem", None, None),
        P("mem", None, None),
        P("grp", None),
        P("grp", None, "mem"),
        P("grp", None, "mem"),
        P("grp", "mem", None),
        P("grp", "mem", None, None),
        P("grp", "mem"),
    )
    out_specs = (
        P("grp", "mem", None, None),
        P("mem", None, None),
        P("mem", None, None),
        P("mem", None, None),
        P("grp", None, "mem"),
        P("grp", None, "mem"),
        P("grp", "mem", None),
    )
    return jax.shard_map(
        on_device, mesh=mesh, in_specs=in_specs, out_specs=out_specs, check_vma=False
    )
```

profile of v0, /device:TPU:1, one launch (start us, length us, event | category | flops | bytes accessed | tf_op | source)
XLA Modules:
  0.0 137.6 jit_solution(7572657574202410857)
XLA Ops:
  1.5 0.5 iota_compare_fusion.2
  2.0 1.1 fusion.34
  3.1 0.7 reduce
  3.8 1.4 %convolution_convert_fusion.3 = bf16[128,256]{1,0:T(8,128)(2,1)S(1)} fusion(bf16[1,896,256]{2,1,0:T(8,128)(2,1)} %param.14, bf16[1,1,128,896]{3,2,1,0:T(8,128)(2,1)} %param.11, f32[896]{0:T(1024)S(1)} %reduce, f32[128]{0:T(128)S(1)} %add_rsqrt_fusion), kind=kOutput, calls=%fused_computation.18 | convolution fusion | flops 59211776 | bytes 757760 | tf_op jit(solution)/shard_map/dot_general | solution.py:474
  5.3 0.6 fusion.44
  6.0 0.9 copy.31
  6.9 1.7 %bitcast_select_fusion.1.cot_own = bf16[128,896]{1,0:T(8,128)(2,1)} fusion(bf16[1,1,128,896]{3,2,1,0:T(8,128)(2,1)} %param.20, pred[128]{0:T(512)(128)(4,1)} %iota_compare_fusion.2), kind=kLoop, calls=%fused_computation.53 | loop fusion | flops 114688 | bytes 458880 | tf_op jit(solution)/shard_map/jit(_where)/select_n | solution.py:469
  8.7 1.9 %fusion.9 = bf16[128,896]{1,0:T(8,128)(2,1)} fusion(bf16[1,896,896]{2,1,0:T(8,128)(2,1)S(1)} %copy-done.7, bf16[1,1,128,896]{3,2,1,0:T(8,128)(2,1)S(1)} %copy-done.1, f32[896]{0:T(1024)} %copy-done.10, f32[128]{0:T(128)} %copy-done.12), kind=kOutput, calls=%fused_computation.13 | convolution fusion | flops 206094336 | bytes 2068480 | tf_op jit(solution)/shard_map/dot_general | solution.py:473
  10.5 1.1 copy.33
  11.7 0.8 fusion.36.normed_own
  13.0 0.6 multiply_divide_fusion
  14.1 0.8 copy.35.attended_own
  14.9 1.2 fusion.15.cut_own
  16.1 53.8 %server.1 = (bf16[128,896]{1,0:T(8,128)(2,1)}, bf16[128,896]{1,0:T(8,128)(2,1)}, bf16[8,128,896]{2,1,0:T(8,128)(2,1)}, bf16[8,128,896]{2,1,0:T(8,128)(2,1)}, bf1...) custom-call(bf16[128,896]{1,0:T(8,128)(2,1)} %fusion.15.cut_own, ...), custom_call_target="tpu_custom_call" | custom-call | tf_op jit(solution)/shard_map/server/pallas_call | solution.py:289
  69.8 1.6 %constant_dynamic-slice_fusion.half_own = bf16[64,896]{1,0:T(8,128)(2,1)} fusion(bf16[128,896]{1,0:T(8,128)(2,1)} %get-tuple-element.22, s32[]{:T(128)S(6)} %select_n.31), kind=kLoop, calls=%fused_computation.61 | loop fusion | bytes 229380 | tf_op jit(solution)/shard_map/dynamic_slice | solution.py:487
  71.4 1.5 %fusion.12 = bf16[128,896]{1,0:T(8,128)(2,1)S(1)} fusion(bf16[128,896]{1,0:T(8,128)(2,1)} %get-tuple-element.22, bf16[1,896,896]{2,1,0:T(8,128)(2,1)S(1)} %copy-done), kind=kOutput, calls=%fused_computation.14 | convolution fusion | flops 205635584 | bytes 2064384 | tf_op jit(solution)/shard_map/dot_general | solution.py:483
  73.1 0.4 fusion.18
  73.7 1.1 fusion.27
  74.8 0.4 fusion.30
  75.3 0.4 fusion.25
  76.6 0.7 pad_maximum_fusion.d_own
  77.3 46.6 %grads.1 = (bf16[896,1152]{1,0:T(8,128)(2,1)}, bf16[896,896]{1,0:T(8,128)(2,1)}, bf16[1216,896]{1,0:T(8,128)(2,1)}, bf16[1216,896]{1,0:T(8,128)(2,1)}, bf16[1216,896]{1,0:T(8,128)(2,1)}) custom-call(bf16[128,1152]{1,0:T(8,128)(2,1)} %pad_maximum_fusion.d_own, bf16[64,896]{1,0:T(8,128)(2,1)} %constant_dynamic-slice_fusion.half_own, ...), custom_call_target="tpu_custom_call" | custom-call | tf_op jit(solution)/shard_map/grads/pallas_call | solution.py:423
  123.9 1.8 %slice_bitcast_fusion.1 = bf16[1,896,256]{2,1,0:T(8,128)(2,1)} fusion(bf16[896,1152]{1,0:T(8,128)(2,1)} %get-tuple-element.30), kind=kLoop, calls=%fused_computation.49 | loop fusion | bytes 917504 | tf_op jit(solution)/shard_map/broadcast_in_dim | solution.py:494
  125.7 2.8 %slice_bitcast_fusion = bf16[1,896,896]{2,1,0:T(8,128)(2,1)} fusion(bf16[896,1152]{1,0:T(8,128)(2,1)} %get-tuple-element.30), kind=kLoop, calls=%fused_computation.6 | loop fusion | bytes 3211264 | tf_op jit(solution)/shard_map/broadcast_in_dim | solution.py:493
  128.6 0.7 copy.53
  129.3 1.2 copy.54
  130.4 1.0 copy-done.4
  131.5 1.3 copy.55
  132.8 1.1 copy-done.3
  133.9 1.3 copy.56
  135.2 1.1 copy-done.2
  136.3 1.3 copy.57
  (42 shorter events, 2.3 us)
Async XLA Ops:
  0.6 14.3 %copy-start = (bf16[1,896,896]{2,1,0:T(8,128)(2,1)S(1)}, bf16[1,896,896]{2,1,0:T(8,128)(2,1)}, u32[]{:S(2)}) copy-start(bf16[1,896,896]{2,1,0:T(8,128)(2,1)} %param.15) | copy-start | bytes 4816900
  0.6 8.0 %copy-start.1 = (bf16[1,1,128,896]{3,2,1,0:T(8,128)(2,1)S(1)}, bf16[1,1,128,896]{3,2,1,0:T(8,128)(2,1)}, u32[]{:S(2)}) copy-start(bf16[1,1,128,896]{3,2,1,0:T(8,128)(2,1)} %param.11) | copy-start | bytes 688132
  0.7 8.0 %copy-start.7 = (bf16[1,896,896]{2,1,0:T(8,128)(2,1)S(1)}, bf16[1,896,896]{2,1,0:T(8,128)(2,1)}, u32[]{:S(2)}) copy-start(bf16[1,896,896]{2,1,0:T(8,128)(2,1)} %param.13) | copy-start | bytes 4816900
  3.1 2.8 %copy-start.12 = (f32[128]{0:T(128)}, f32[128]{0:T(128)S(1)}, u32[]{:S(2)}) copy-start(f32[128]{0:T(128)S(1)} %add_rsqrt_fusion) | copy-start | bytes 1540
  3.8 2.1 %copy-start.10 = (f32[896]{0:T(1024)}, f32[896]{0:T(1024)S(1)}, u32[]{:S(2)}) copy-start(f32[896]{0:T(1024)S(1)} %reduce) | copy-start | bytes 10756
  6.0 5.6 %copy-start.11 = (f32[896]{0:T(1024)S(1)}, f32[896]{0:T(1024)}, u32[]{:S(2)}) copy-start(f32[896]{0:T(1024)} %copy-done.10) | copy-start | bytes 10756
  6.0 5.6 %copy-start.13 = (f32[128]{0:T(128)S(1)}, f32[128]{0:T(128)}, u32[]{:S(2)}) copy-start(f32[128]{0:T(128)} %copy-done.12) | copy-start | bytes 1540
  11.6 1.4 copy-start.5
  74.8 0.9 copy-start.6
  125.7 2.8 %copy-start.9 = (bf16[128,896]{1,0:T(8,128)(2,1)S(1)}, bf16[128,896]{1,0:T(8,128)(2,1)}, u32[]{:S(2)}) copy-start(bf16[128,896]{1,0:T(8,128)(2,1)} %get-tuple-element.21) | copy-start | bytes 688132
  125.7 3.5 %copy-start.8 = (bf16[896,896]{1,0:T(8,128)(2,1)S(1)}, bf16[896,896]{1,0:T(8,128)(2,1)}, u32[]{:S(2)}) copy-start(bf16[896,896]{1,0:T(8,128)(2,1)} %get-tuple-element.31) | copy-start | bytes 4816900
  129.3 2.2 %copy-start.4 = (bf16[1216,896]{1,0:T(8,128)(2,1)S(1)}, bf16[1216,896]{1,0:T(8,128)(2,1)}, u32[]{:S(2)}) copy-start(bf16[1216,896]{1,0:T(8,128)(2,1)} %get-tuple-element.32) | copy-start | bytes 6537220
  131.5 2.4 %copy-start.3 = (bf16[1216,896]{1,0:T(8,128)(2,1)S(1)}, bf16[1216,896]{1,0:T(8,128)(2,1)}, u32[]{:S(2)}) copy-start(bf16[1216,896]{1,0:T(8,128)(2,1)} %get-tuple-element.33) | copy-start | bytes 6537220
  133.9 2.4 %copy-start.2 = (bf16[1216,896]{1,0:T(8,128)(2,1)S(1)}, bf16[1216,896]{1,0:T(8,128)(2,1)}, u32[]{:S(2)}) copy-start(bf16[1216,896]{1,0:T(8,128)(2,1)} %get-tuple-element.34) | copy-start | bytes 6537220
where the time goes:
time: 140 us; the launch traced here: 138 us
  Pallas kernels  100 us (71%)
  local copies, waits for them, and re-layouts  19.4 us (14%)
  matrix products  8.59 us (6%)
  other arithmetic  7.5 us (5%)
  between operations  1.72 us (1%)
    pallas_call x1, Pallas kernels, server_call(): pl.pallas_call(server_kernel, out_shape=[shape((length, width), BF16), sh...  53.8 us
    pallas_call x1, Pallas kernels, grads_call(): pl.pallas_call(grads_kernel, out_shape=[shape((width, wide), BF16), shape...  46.6 us
    unnamed x33, local copies, waits for them, and re-layouts  9.12 us
    broadcast_in_dim x1, local copies, waits for them, and re-layouts, on_device(): grad_in[None, :, :queries.shape[1]]  2.83 us

commit v1 on v0

--- a/solution.py
+++ b/solution.py
@@ -49,13 +49,16 @@
 
 
 class Gather:
-    def __init__(self, axis, own, slots, sems):
+    def __init__(self, axis, own, slots, sems, split=False):
         self.axis, self.own, self.slots, self.sems = axis, own, slots, sems
+        self.taken = set()
         self.n = lax.axis_size(axis)
         self.pairs = self.n // 2
         me = lax.axis_index(axis)
         self.right = {axis: lax.rem(me + 2, self.n)}
         self.partner = {axis: me + 1 - 2 * lax.rem(me, 2)}
+        self.split = split and self.pairs > 1
+        self.cut_at = own.shape[0] // 2
 
     def source(self, step):
         return self.own if step == 0 else self.slots.at[2 * step]
@@ -71,10 +74,26 @@
             device_id_type=MESH,
         )
 
+    def rest_copy(self):
+        rows = pl.ds(self.cut_at, self.own.shape[0] - self.cut_at)
+        last = 2 * self.pairs - 1
+        return pltpu.make_async_remote_copy(
+            src_ref=self.slots.at[last - 2, rows],
+            dst_ref=self.slots.at[last, rows],
+            send_sem=self.sems[0].at[self.pairs - 1],
+            recv_sem=self.sems[1].at[self.pairs - 1],
+            device_id=self.right,
+            device_id_type=MESH,
+        )
+
     def flip_copy(self, step):
+        src, dst = self.source(step), self.slots.at[2 * step + 1]
+        if self.split and step == self.pairs - 1:
+            rows = pl.ds(0, self.cut_at)
+            src, dst = self.slots.at[2 * step, rows], self.slots.at[2 * step + 1, rows]
         return pltpu.make_async_remote_copy(
-            src_ref=self.source(step),
-            dst_ref=self.slots.at[2 * step + 1],
+            src_ref=src,
+            dst_ref=dst,
             send_sem=self.sems[2].at[step],
             recv_sem=self.sems[3].at[step],
             device_id=self.partner,
@@ -87,22 +106,32 @@
         if step < self.pairs - 1:
             self.ring_copy(step).start()
         self.flip_copy(step).start()
+        if self.split and step == self.pairs - 1:
+            self.take(step - 1)
+            self.rest_copy().start()
 
     def take(self, step):
+        if step in self.taken:
+            return
+        self.taken.add(step)
         self.flip_copy(step).wait_recv()
+        if self.split and step == self.pairs - 1:
+            self.rest_copy().wait_recv()
 
     def finish(self):
         for step in range(self.pairs):
             if step < self.pairs - 1:
                 self.ring_copy(step).wait_send()
             self.flip_copy(step).wait_send()
+        if self.split:
+            self.rest_copy().wait_send()
 
 
 def gather_sems(n):
     pairs = n // 2
     return [
-        pltpu.SemaphoreType.DMA((max(pairs - 1, 1),)),
-        pltpu.SemaphoreType.DMA((max(pairs - 1, 1),)),
+        pltpu.SemaphoreType.DMA((pairs,)),
+        pltpu.SemaphoreType.DMA((pairs,)),
         pltpu.SemaphoreType.DMA((pairs,)),
         pltpu.SemaphoreType.DMA((pairs,)),
     ]
@@ -138,7 +167,9 @@
 
 def server_kernel(
     cut_own, cot_own, attended_own, normed_own, gain, gate_hbm, up_hbm, down_hbm,
-    server_out, cut_grad, attended_all, normed_all, rows_normed, rows_cot, hidden, d_gate, d_up,
+    server_out, cut_grad, attended_far, normed_far, rows_normed_far, rows_cot_far,
+    hidden_far, d_gate_far, d_up_far,
+    attended_all, normed_all, rows_normed, rows_cot, hidden, d_gate, d_up, store_sem,
     gate_w, up_w, down_w, cut_slots, served, served_in, home_in, home_out, sums, give, give_in,
     passing, pass_in, load_sem, cut_sems, cot_sems, attended_sems, normed_sems, swap_sems, part_sems,
     home_sems, pass_sems,
@@ -158,8 +189,8 @@
     cut = Gather("mem", cut_own, cut_slots, cut_sems)
     cot = Gather("mem", cot_own, rows_cot, cot_sems)
     early = [
-        Gather("grp", normed_own, normed_all, normed_sems),
-        Gather("grp", attended_own, attended_all, attended_sems),
+        Gather("grp", normed_own, normed_all, normed_sems, True),
+        Gather("grp", attended_own, attended_all, attended_sems, True),
     ]
     cut.advance(0)
     cot.advance(0)
@@ -171,7 +202,18 @@
     attended_all[0] = attended_own[...]
     sums[...] = cot_own[...].astype(F32)
     swaps = []
-    group_step = 1
+    pending = [(chain, step) for step in range(1, group_pairs) for chain in early]
+    stores = []
+
+    def keep_going():
+        if pending:
+            chain, step = pending.pop(0)
+            chain.advance(step)
+
+    def store(near, far):
+        stores.append(pltpu.make_async_copy(near, far, store_sem.at[len(stores)]))
+        stores[-1].start()
+
     for p in range(pairs):
         if p > 0:
             cut.advance(p)
@@ -192,6 +234,7 @@
         )
         gate_act = lax.dot_general(normed, gate_w[...], CONTRACT_LAST, preferred_element_type=F32)
         up_act = lax.dot_general(normed, up_w[...], CONTRACT_LAST, preferred_element_type=F32)
+        keep_going()
         sigma = jax.nn.sigmoid(gate_act)
         acted = gate_act * sigma
         hidden_now = (acted * up_act).astype(BF16)
@@ -210,10 +253,13 @@
             .astype(BF16)
             .reshape(2, length, width)
         )
-        if group_step < group_pairs - 1:
-            for chain in early:
-                chain.advance(group_step)
-            group_step += 1
+        keep_going()
+        for near, far in (
+            (hidden, hidden_far), (d_gate, d_gate_far), (d_up, d_up_far)
+        ):
+            store(near.at[rows], far.at[rows])
+        store(rows_normed.at[span], rows_normed_far.at[span])
+        store(rows_cot.at[span], rows_cot_far.at[span])
 
     keep_rows = pl.ds(pl.multiple_of(odd * half, half), half)
     give_rows = pl.ds(pl.multiple_of((1 - odd) * half, half), half)
@@ -224,6 +270,7 @@
         swaps.append(send(served.at[2 * p + 1], served_in.at[p], swap_sems, p, partner))
         swaps[-1].start()
     handed.wait_recv()
+    keep_going()
     total = sums[keep_rows] + give_in[...].astype(F32)
     passing[...] = total.astype(BF16)
     passes = []
@@ -259,14 +306,16 @@
         homes[p - 1].wait_recv()
         result = result + home_in[p - 1].astype(F32)
     server_out[...] = result.astype(BF16)
-    while group_step < group_pairs:
-        for chain in early:
-            chain.advance(group_step)
-        group_step += 1
-    for chain in early:
+    while pending:
+        keep_going()
+    for chain, far in zip(early, (normed_far, attended_far)):
         for step in range(group_pairs):
             chain.take(step)
+        store(chain.slots, far)
+    for chain in early:
         chain.finish()
+    for copy in stores:
+        copy.wait()
     cut.finish()
     cot.finish()
     back.wait_recv()
@@ -300,8 +349,16 @@
             shape((rows, units), BF16),
         ],
         in_specs=[vmem] * 5 + [far] * 3,
-        out_specs=[vmem] * 9,
+        out_specs=[vmem] * 2 + [far] * 7,
         scratch_shapes=[
+            pltpu.VMEM((groups, length, width), BF16),
+            pltpu.VMEM((groups, length, width), BF16),
+            pltpu.VMEM((members, length, width), BF16),
+            pltpu.VMEM((members, length, width), BF16),
+            pltpu.VMEM((rows, units), BF16),
+            pltpu.VMEM((rows, units), BF16),
+            pltpu.VMEM((rows, units), BF16),
+            pltpu.SemaphoreType.DMA((5 * pairs + 2,)),
             pltpu.VMEM((units, width), BF16),
             pltpu.VMEM((units, width), BF16),
             pltpu.VMEM((units, width), BF16),
@@ -333,9 +390,12 @@
 
 
 def grads_kernel(
-    d_own, half_own, attended_all, normed_all, rows_normed, rows_cot, hidden, d_gate, d_up,
-    grad_in, grad_out, grad_gate, grad_up, grad_down,
-    d_slots, half_slots, half_in, acc, d_sems, half_sems, swap_sems,
+    d_own, half_own, attended_far, normed_far, rows_normed_far, rows_cot_far,
+    hidden_far, d_gate_far, d_up_far,
+    grad_query, grad_keyval, grad_out, grad_gate_far, grad_up_far, grad_down_far,
+    attended_all, normed_all, rows_normed, rows_cot, hidden, d_gate, d_up,
+    grad_gate, grad_up, grad_down,
+    d_slots, half_slots, half_in, acc, d_sems, half_sems, swap_sems, load_sem, store_sem,
 ):
     groups = lax.axis_size("grp")
     group_pairs = groups // 2
@@ -345,47 +405,66 @@
     me = lax.axis_index("mem")
     odd = lax.rem(me, 2)
     partner = {"mem": me + 1 - 2 * odd}
+    loads = []
+    for i, (far, near) in enumerate((
+        (hidden_far, hidden), (rows_cot_far, rows_cot), (d_gate_far, d_gate),
+        (rows_normed_far, rows_normed), (d_up_far, d_up), (normed_far, normed_all),
+        (attended_far, attended_all),
+    )):
+        loads.append(pltpu.make_async_copy(far, near, load_sem.at[i]))
+        loads[-1].start()
     greet(("grp", "mem"))
-    halves = Gather("grp", half_own, half_slots, half_sems)
-    deltas = Gather("grp", d_own, d_slots, d_sems)
+    halves = Gather("grp", half_own, half_slots, half_sems, True)
+    deltas = Gather("grp", d_own, d_slots, d_sems, True)
     chains = [halves, deltas]
     for chain in chains:
         chain.advance(0)
     half_slots[0] = half_own[...]
     d_slots[0] = d_own[...]
-    acc_rows = acc.shape[0] // 2
+    pending = [(chain, step) for step in range(1, group_pairs) for chain in chains]
+
+    def keep_going():
+        if pending:
+            chain, step = pending.pop(0)
+            chain.advance(step)
 
     def weight_grad(left, right, out):
-        right_now = right
-        units = out.shape[0]
         out[...] = lax.dot_general(
-            left[...], right_now, CONTRACT_FIRST, preferred_element_type=F32
+            left[...], right[...].reshape(rows, width), CONTRACT_FIRST, preferred_element_type=F32
         ).astype(BF16)
 
-    cot = rows_cot[...].reshape(rows, width)
-    normed = rows_normed[...].reshape(rows, width)
-    jobs = [(hidden, cot, grad_down), (d_gate, normed, grad_gate), (d_up, normed, grad_up)]
-    for step in range(1, group_pairs):
-        if jobs:
-            weight_grad(*jobs.pop(0))
-        for chain in chains:
-            chain.advance(step)
-    while jobs:
-        weight_grad(*jobs.pop(0))
+    for load in loads:
+        load.wait()
+    stores = []
+    for i, (left, right, near, far) in enumerate((
+        (hidden, rows_cot, grad_down, grad_down_far),
+        (d_gate, rows_normed, grad_gate, grad_gate_far),
+        (d_up, rows_normed, grad_up, grad_up_far),
+    )):
+        weight_grad(left, right, near)
+        stores.append(pltpu.make_async_copy(near, far, store_sem.at[i]))
+        stores[-1].start()
+        keep_going()
+    while pending:
+        keep_going()
+
+    def grad_in(first, count):
+        return lax.dot_general(
+            normed_all[pl.ds(first, count)].reshape(count * length, width),
+            d_slots[pl.ds(first, count)].reshape(count * length, d_slots.shape[2]),
+            CONTRACT_FIRST,
+            preferred_element_type=F32,
+        )
+
+    scale = 1.0 / groups
+    ready = groups - 2
+    for step in range(group_pairs - 1):
+        deltas.take(step)
+    acc[...] = grad_in(0, ready)
     for step in range(group_pairs):
         halves.take(step)
     swap = send(half_slots, half_in, swap_sems, 0, partner)
     swap.start()
-    ready = groups - 2
-    for step in range(group_pairs - 1):
-        deltas.take(step)
-    scale = 1.0 / groups
-    acc[...] = lax.dot_general(
-        normed_all[pl.ds(0, ready)].reshape(ready * length, width),
-        d_slots[pl.ds(0, ready)].reshape(ready * length, d_slots.shape[2]),
-        CONTRACT_FIRST,
-        preferred_element_type=F32,
-    )
     swap.wait_recv()
     mine = half_slots[...]
     other = half_in[...]
@@ -401,37 +480,43 @@
     )
     grad_out[...] = (out * scale).astype(BF16)
     deltas.take(group_pairs - 1)
-    last = lax.dot_general(
-        normed_all[pl.ds(ready, 2)].reshape(2 * length, width),
-        d_slots[pl.ds(ready, 2)].reshape(2 * length, d_slots.shape[2]),
-        CONTRACT_FIRST,
-        preferred_element_type=F32,
-    )
-    grad_in[...] = ((acc[...] + last) * scale).astype(BF16)
+    split = grad_query.shape[1]
+    result = (acc[...] + grad_in(ready, 2)) * scale
+    grad_query[...] = result[:, :split].astype(BF16)
+    grad_keyval[...] = result[:, split:].astype(BF16)
     for chain in chains:
         chain.finish()
     swap.wait_send()
-
-
-def grads_call(d_own, half_own, attended_all, normed_all, rows_normed, rows_cot, hidden, d_gate, d_up):
+    for copy in stores:
+        copy.wait()
+
+
+def grads_call(
+    columns, d_own, half_own, attended_all, normed_all, rows_normed, rows_cot, hidden, d_gate, d_up
+):
     groups = lax.axis_size("grp")
     half, width = half_own.shape
     length, wide = d_own.shape
     units = hidden.shape[1]
     shape = jax.ShapeDtypeStruct
     vmem = pl.BlockSpec(memory_space=pltpu.VMEM)
+    far = pl.BlockSpec(memory_space=pl.ANY)
+    wide_operands = [attended_all, normed_all, rows_normed, rows_cot, hidden, d_gate, d_up]
     return pl.pallas_call(
         grads_kernel,
         out_shape=[
-            shape((width, wide), BF16),
+            shape((width, columns), BF16),
+            shape((width, wide - columns), BF16),
             shape((width, width), BF16),
             shape((units, width), BF16),
             shape((units, width), BF16),
             shape((units, width), BF16),
         ],
-        in_specs=[vmem] * 9,
-        out_specs=[vmem] * 5,
-        scratch_shapes=[
+        in_specs=[vmem] * 2 + [far] * 7,
+        out_specs=[vmem] * 3 + [far] * 3,
+        scratch_shapes=[pltpu.VMEM(a.shape, BF16) for a in wide_operands]
+        + [pltpu.VMEM((units, width), BF16)] * 3
+        + [
             pltpu.VMEM((groups, length, wide), BF16),
             pltpu.VMEM((groups, half, width), BF16),
             pltpu.VMEM((groups, half, width), BF16),
@@ -439,12 +524,14 @@
             gather_sems(groups),
             gather_sems(groups),
             [pltpu.SemaphoreType.DMA((1,))] * 2,
+            pltpu.SemaphoreType.DMA((7,)),
+            pltpu.SemaphoreType.DMA((3,)),
         ],
         compiler_params=pltpu.CompilerParams(
             collective_id=1, has_side_effects=True, vmem_limit_bytes=60 * 2**20
         ),
         name="grads",
-    )(d_own, half_own, attended_all, normed_all, rows_normed, rows_cot, hidden, d_gate, d_up)
+    )(d_own, half_own, *wide_operands)
 
 
 def on_device(
@@ -485,13 +572,13 @@
     ).astype(BF16)
     d_queries, d_key_vals = pull(d_attended)
     half_grad = lax.dynamic_slice_in_dim(cut_grad, odd * half, half, 0)
-    grad_in, grad_out, grad_gate, grad_up, grad_down = grads_call(
-        jnp.concatenate([d_queries, d_key_vals], axis=1), half_grad, attended_all, normed_all, *rest
+    grad_query, grad_keyval, grad_out, grad_gate, grad_up, grad_down = grads_call(
+        queries.shape[1], jnp.concatenate([d_queries, d_key_vals], axis=1), half_grad, attended_all, normed_all, *rest
     )
     return (
         server_out[None, None],
-        grad_in[None, :, : queries.shape[1]],
-        grad_in[None, :, queries.shape[1] :],
+        grad_query[None],
+        grad_keyval[None],
         grad_out[None],
         grad_gate.T[None],
         grad_up.T[None],

time: 140 us -> 126 us (0.900); the launches traced: 138 us -> 125 us
  Pallas kernels: 100 us -> 89.1 us
    pallas_call x1, Pallas kernels: 53.8 us -> 45.2 us  [server_call(): pl.pallas_call(server_kernel, out_shape=[shape((length, width), BF16), sh...]
    broadcast_in_dim x2 -> x0, local copies, waits for them, and re-layouts: 4.65 us -> none  [the longest x1 2.83 us: on_device(): grad_in[None, :, :queries.shape[1]]]
    unnamed x33 -> x37, local copies, waits for them, and re-layouts: 9.12 us -> 12.7 us
    pallas_call x1, Pallas kernels: 46.6 us -> 43.9 us  [grads_call(): pl.pallas_call(grads_kernel, out_shape=[shape((width, columns), BF16), sh...]
where the time goes in v1:
time: 126 us; the launch traced here: 125 us
  Pallas kernels  89.1 us (71%)
  local copies, waits for them, and re-layouts  18.6 us (15%)
  matrix products  8.44 us (7%)
  other arithmetic  7.5 us (6%)
  between operations  1.73 us (1%)
    pallas_call x1, Pallas kernels, server_call(): pl.pallas_call(server_kernel, out_shape=[shape((length, width), BF16), sh...  45.2 us
    pallas_call x1, Pallas kernels, grads_call(): pl.pallas_call(grads_kernel, out_shape=[shape((width, columns), BF16), sh...  43.9 us
    unnamed x37, local copies, waits for them, and re-layouts  12.7 us

profile of v1, /device:TPU:1, one launch (start us, length us, event | category | flops | bytes accessed | tf_op | source)
XLA Modules:
  0.0 125.4 jit_solution(13216282635848844150)
XLA Ops:
  1.5 0.5 iota_compare_fusion.2
  2.0 1.1 fusion.34
  3.1 0.7 reduce
  3.8 1.4 %convolution_convert_fusion.3 = bf16[128,256]{1,0:T(8,128)(2,1)S(1)} fusion(bf16[1,896,256]{2,1,0:T(8,128)(2,1)} %param.14, bf16[1,1,128,896]{3,2,1,0:T(8,128)(2,1)} %param.11, f32[896]{0:T(1024)S(1)} %reduce, f32[128]{0:T(128)S(1)} %add_rsqrt_fusion), kind=kOutput, calls=%fused_computation.17 | convolution fusion | flops 59211776 | bytes 757760 | tf_op jit(solution)/shard_map/dot_general | solution.py:561
  5.3 0.6 fusion.44
  6.0 0.9 copy.31
  6.9 1.7 %bitcast_select_fusion.1.cot_own = bf16[128,896]{1,0:T(8,128)(2,1)} fusion(bf16[1,1,128,896]{3,2,1,0:T(8,128)(2,1)} %param.20, pred[128]{0:T(512)(128)(4,1)} %iota_compare_fusion.2), kind=kLoop, calls=%fused_computation.51 | loop fusion | flops 114688 | bytes 458880 | tf_op jit(solution)/shard_map/jit(_where)/select_n | solution.py:556
  8.7 1.9 %fusion.9 = bf16[128,896]{1,0:T(8,128)(2,1)} fusion(bf16[1,896,896]{2,1,0:T(8,128)(2,1)S(1)} %copy-done.7, bf16[1,1,128,896]{3,2,1,0:T(8,128)(2,1)S(1)} %copy-done.1, f32[896]{0:T(1024)} %copy-done.11, f32[128]{0:T(128)} %copy-done.13), kind=kOutput, calls=%fused_computation.12 | convolution fusion | flops 206094336 | bytes 2068480 | tf_op jit(solution)/shard_map/dot_general | solution.py:560
  10.5 1.1 copy.33
  11.7 0.8 fusion.36.normed_own
  13.0 0.6 multiply_divide_fusion
  14.1 0.8 copy.35.attended_own
  14.9 1.2 fusion.15.cut_own
  16.1 45.2 %server.1 = (bf16[128,896]{1,0:T(8,128)(2,1)}, bf16[128,896]{1,0:T(8,128)(2,1)}, bf16[8,128,896]{2,1,0:T(8,128)(2,1)}, bf16[8,128,896]{2,1,0:T(8,128)(2,1)}, bf1...) custom-call(bf16[128,896]{1,0:T(8,128)(2,1)} %fusion.15.cut_own, ...), custom_call_target="tpu_custom_call" | custom-call | tf_op jit(solution)/shard_map/server/pallas_call | solution.py:338
  61.3 1.6 %constant_dynamic-slice_fusion.half_own = bf16[64,896]{1,0:T(8,128)(2,1)} fusion(bf16[128,896]{1,0:T(8,128)(2,1)} %get-tuple-element.23, s32[]{:T(128)S(6)} %select_n.31), kind=kLoop, calls=%fused_computation.59 | loop fusion | bytes 229380 | tf_op jit(solution)/shard_map/dynamic_slice | solution.py:574
  62.9 1.5 %fusion.12 = bf16[128,896]{1,0:T(8,128)(2,1)S(1)} fusion(bf16[128,896]{1,0:T(8,128)(2,1)} %get-tuple-element.23, bf16[1,896,896]{2,1,0:T(8,128)(2,1)S(1)} %copy-done), kind=kOutput, calls=%fused_computation.13 | convolution fusion | flops 205635584 | bytes 2064384 | tf_op jit(solution)/shard_map/dot_general | solution.py:570
  64.4 0.3 copy.36
  65.2 1.1 fusion.27
  66.3 0.4 fusion.30
  66.8 0.4 fusion.25
  68.1 0.7 pad_maximum_fusion.d_own
  68.8 43.9 %grads.1 = (bf16[896,896]{1,0:T(8,128)(2,1)}, bf16[896,256]{1,0:T(8,128)(2,1)}, bf16[896,896]{1,0:T(8,128)(2,1)}, bf16[1216,896]{1,0:T(8,128)(2,1)}, bf16[1216,8...) custom-call(bf16[128,1152]{1,0:T(8,128)(2,1)} %pad_maximum_fusion.d_own, bf16[64,896]{1,0:T(8,128)(2,1)} %constant_dynamic-slice_fusion.half_own, ...), custom_call_target="tpu_custom_call" | custom-call | tf_op jit(solution)/shard_map/grads/pallas_call | solution.py:505
  112.7 0.7 copy.55
  113.4 2.8 %copy.56 = bf16[1,896,896]{2,1,0:T(8,128)(2,1)} copy(bf16[1,896,896]{2,1,0:T(8,128)(2,1)} %bitcast.156) | data formatting | bytes 3211264
  116.3 0.8 copy.57
  117.1 1.2 copy.58
  118.2 1.0 copy-done.4
  119.2 1.3 %copy.59 = bf16[1,896,1216]{1,2,0:T(8,128)(2,1)} copy(bf16[1,896,1216]{1,2,0:T(8,128)(2,1)S(1)} %bitcast.150) | data formatting | bytes 4358144
  120.6 1.1 copy-done.3
  121.6 1.3 %copy.60 = bf16[1,896,1216]{1,2,0:T(8,128)(2,1)} copy(bf16[1,896,1216]{1,2,0:T(8,128)(2,1)S(1)} %bitcast.149) | data formatting | bytes 4358144
  123.0 1.1 copy-done.2
  124.0 1.3 %copy.61 = bf16[1,1216,896]{2,1,0:T(8,128)(2,1)} copy(bf16[1,1216,896]{2,1,0:T(8,128)(2,1)S(1)} %bitcast.148) | data formatting | bytes 4358144
  (44 shorter events, 2.4 us)
Async XLA Ops:
  0.6 14.3 %copy-start = (bf16[1,896,896]{2,1,0:T(8,128)(2,1)S(1)}, bf16[1,896,896]{2,1,0:T(8,128)(2,1)}, u32[]{:S(2)}) copy-start(bf16[1,896,896]{2,1,0:T(8,128)(2,1)} %param.15) | copy-start | bytes 4816900
  0.6 8.0 %copy-start.1 = (bf16[1,1,128,896]{3,2,1,0:T(8,128)(2,1)S(1)}, bf16[1,1,128,896]{3,2,1,0:T(8,128)(2,1)}, u32[]{:S(2)}) copy-start(bf16[1,1,128,896]{3,2,1,0:T(8,128)(2,1)} %param.11) | copy-start | bytes 688132
  0.7 8.0 %copy-start.7 = (bf16[1,896,896]{2,1,0:T(8,128)(2,1)S(1)}, bf16[1,896,896]{2,1,0:T(8,128)(2,1)}, u32[]{:S(2)}) copy-start(bf16[1,896,896]{2,1,0:T(8,128)(2,1)} %param.13) | copy-start | bytes 4816900
  3.1 2.8 %copy-start.13 = (f32[128]{0:T(128)}, f32[128]{0:T(128)S(1)}, u32[]{:S(2)}) copy-start(f32[128]{0:T(128)S(1)} %add_rsqrt_fusion) | copy-start | bytes 1540
  3.8 2.1 %copy-start.11 = (f32[896]{0:T(1024)}, f32[896]{0:T(1024)S(1)}, u32[]{:S(2)}) copy-start(f32[896]{0:T(1024)S(1)} %reduce) | copy-start | bytes 10756
  6.0 5.6 %copy-start.12 = (f32[896]{0:T(1024)S(1)}, f32[896]{0:T(1024)}, u32[]{:S(2)}) copy-start(f32[896]{0:T(1024)} %copy-done.11) | copy-start | bytes 10756
  6.0 5.6 %copy-start.14 = (f32[128]{0:T(128)S(1)}, f32[128]{0:T(128)}, u32[]{:S(2)}) copy-start(f32[128]{0:T(128)} %copy-done.13) | copy-start | bytes 1540
  11.6 1.4 %copy-start.5 = (bf16[128,896]{0,1:T(8,128)(2,1)}, bf16[128,896]{0,1:T(8,128)(2,1)S(1)}, u32[]{:S(2)}) copy-start(bf16[128,896]{0,1:T(8,128)(2,1)S(1)} %copy.33) | copy-start | bytes 688132
  66.3 0.9 copy-start.6
  68.8 43.9 %copy-start.10 = (bf16[128,896]{1,0:T(8,128)(2,1)S(1)}, bf16[128,896]{1,0:T(8,128)(2,1)}, u32[]{:S(2)}) copy-start(bf16[128,896]{1,0:T(8,128)(2,1)} %get-tuple-element.22) | copy-start | bytes 688132
  113.4 2.9 %copy-start.9 = (bf16[896,256]{1,0:T(8,128)(2,1)S(1)}, bf16[896,256]{1,0:T(8,128)(2,1)}, u32[]{:S(2)}) copy-start(bf16[896,256]{1,0:T(8,128)(2,1)} %get-tuple-element.32) | copy-start | bytes 1376260
  113.4 3.6 %copy-start.8 = (bf16[896,896]{1,0:T(8,128)(2,1)S(1)}, bf16[896,896]{1,0:T(8,128)(2,1)}, u32[]{:S(2)}) copy-start(bf16[896,896]{1,0:T(8,128)(2,1)} %get-tuple-element.33) | copy-start | bytes 4816900
  117.0 2.2 %copy-start.4 = (bf16[1216,896]{1,0:T(8,128)(2,1)S(1)}, bf16[1216,896]{1,0:T(8,128)(2,1)}, u32[]{:S(2)}) copy-start(bf16[1216,896]{1,0:T(8,128)(2,1)} %get-tuple-element.34) | copy-start | bytes 6537220
  119.2 2.4 %copy-start.3 = (bf16[1216,896]{1,0:T(8,128)(2,1)S(1)}, bf16[1216,896]{1,0:T(8,128)(2,1)}, u32[]{:S(2)}) copy-start(bf16[1216,896]{1,0:T(8,128)(2,1)} %get-tuple-element.35) | copy-start | bytes 6537220
  121.6 2.4 %copy-start.2 = (bf16[1216,896]{1,0:T(8,128)(2,1)S(1)}, bf16[1216,896]{1,0:T(8,128)(2,1)}, u32[]{:S(2)}) copy-start(bf16[1216,896]{1,0:T(8,128)(2,1)} %get-tuple-element.36) | copy-start | bytes 6537220

commit v2 on v1

--- a/solution.py
+++ b/solution.py
@@ -1,3 +1,5 @@
+import functools
+
 import jax
 import jax.numpy as jnp
 from jax import lax
@@ -390,7 +392,7 @@
 
 
 def grads_kernel(
-    d_own, half_own, attended_far, normed_far, rows_normed_far, rows_cot_far,
+    d_own, cut_own, attended_far, normed_far, rows_normed_far, rows_cot_far,
     hidden_far, d_gate_far, d_up_far,
     grad_query, grad_keyval, grad_out, grad_gate_far, grad_up_far, grad_down_far,
     attended_all, normed_all, rows_normed, rows_cot, hidden, d_gate, d_up,
@@ -399,11 +401,12 @@
 ):
     groups = lax.axis_size("grp")
     group_pairs = groups // 2
-    half, width = half_own.shape
-    length = 2 * half
+    length, width = cut_own.shape
+    half = length // 2
     rows = rows_cot.shape[0] * length
     me = lax.axis_index("mem")
     odd = lax.rem(me, 2)
+    half_own = cut_own.at[pl.ds(pl.multiple_of(odd * half, half), half)]
     partner = {"mem": me + 1 - 2 * odd}
     loads = []
     for i, (far, near) in enumerate((
@@ -492,11 +495,11 @@
 
 
 def grads_call(
-    columns, d_own, half_own, attended_all, normed_all, rows_normed, rows_cot, hidden, d_gate, d_up
+    columns, d_own, cut_grad, attended_all, normed_all, rows_normed, rows_cot, hidden, d_gate, d_up
 ):
     groups = lax.axis_size("grp")
-    half, width = half_own.shape
-    length, wide = d_own.shape
+    width, (length, wide) = cut_grad.shape[1], d_own.shape
+    half = length // 2
     units = hidden.shape[1]
     shape = jax.ShapeDtypeStruct
     vmem = pl.BlockSpec(memory_space=pltpu.VMEM)
@@ -531,7 +534,45 @@
             collective_id=1, has_side_effects=True, vmem_limit_bytes=60 * 2**20
         ),
         name="grads",
-    )(d_own, half_own, *wide_operands)
+    )(d_own, cut_grad, *wide_operands)
+
+
+def hand_over_kernel(count, *refs):
+    fars, outs, nears = refs[:count], refs[count : 2 * count], refs[2 * count : 3 * count]
+    load_sem, store_sem = refs[3 * count :]
+    pieces = []
+    for far, out, near in zip(fars, outs, nears):
+        rows = far.shape[0]
+        parts = 2 if rows % 32 == 0 else 1
+        for part in range(parts):
+            span = pl.ds(part * (rows // parts), rows // parts)
+            i = len(pieces)
+            pieces.append((
+                pltpu.make_async_copy(far.at[span], near.at[span], load_sem.at[i]),
+                pltpu.make_async_copy(near.at[span], out.at[span], store_sem.at[i]),
+            ))
+    for load, _ in pieces:
+        load.start()
+    for load, store in pieces:
+        load.wait()
+        store.start()
+    for _, store in pieces:
+        store.wait()
+
+
+def hand_over(arrays):
+    far = pl.BlockSpec(memory_space=pl.ANY)
+    count = len(arrays)
+    return pl.pallas_call(
+        functools.partial(hand_over_kernel, count),
+        out_shape=[jax.ShapeDtypeStruct(a.shape, a.dtype) for a in arrays],
+        in_specs=[far] * count,
+        out_specs=[far] * count,
+        scratch_shapes=[pltpu.VMEM(a.shape, a.dtype) for a in arrays]
+        + [pltpu.SemaphoreType.DMA((2 * count,))] * 2,
+        compiler_params=pltpu.CompilerParams(vmem_limit_bytes=60 * 2**20),
+        name="results",
+    )(*arrays)
 
 
 def on_device(
@@ -550,8 +591,6 @@
     tokens_in = client_input[0, 0]
     output_w = w_out[0]
     length, width = tokens_in.shape
-    half = length // 2
-    odd = lax.axis_index("mem") % 2
     live = jnp.arange(length) < valid[0, 0]
     own_cot = jnp.where(live[:, None], out_grad[0, 0], jnp.zeros_like(out_grad[0, 0]))
 
@@ -571,9 +610,11 @@
         cut_grad, output_w, CONTRACT_LAST, preferred_element_type=F32
     ).astype(BF16)
     d_queries, d_key_vals = pull(d_attended)
-    half_grad = lax.dynamic_slice_in_dim(cut_grad, odd * half, half, 0)
     grad_query, grad_keyval, grad_out, grad_gate, grad_up, grad_down = grads_call(
-        queries.shape[1], jnp.concatenate([d_queries, d_key_vals], axis=1), half_grad, attended_all, normed_all, *rest
+        queries.shape[1], jnp.concatenate([d_queries, d_key_vals], axis=1), cut_grad, attended_all, normed_all, *rest
+    )
+    (server_out, grad_query, grad_keyval, grad_out, grad_gate, grad_up, grad_down) = hand_over(
+        [server_out, grad_query, grad_keyval, grad_out, grad_gate, grad_up, grad_down]
     )
     return (
         server_out[None, None],

time: 126 us -> 117 us (0.929)
  local copies, waits for them, and re-layouts: 18.6 us -> 1.86 us
  Pallas kernels: 89.1 us -> 97.4 us
    unnamed x37 -> x8, local copies, waits for them, and re-layouts: 12.7 us -> 0.06 us
    pallas_call x0 -> x1, Pallas kernels: none -> 8.26 us  [hand_over(): pl.pallas_call(functools.partial(hand_over_kernel, count), out_shape=[jax...]
    dynamic_slice x1 -> x0, local copies, waits for them, and re-layouts: 1.56 us -> none  [on_device(): half_grad = lax.dynamic_slice_in_dim(cut_grad, odd * half, half, 0)]
where the time goes in v2:
time: 117 us
  Pallas kernels  97.4 us (83%)
  matrix products  8.66 us (7%)
  other arithmetic  6.99 us (6%)
  local copies, waits for them, and re-layouts  1.86 us (2%)
  between operations  1.8 us (2%)
    pallas_call x1, Pallas kernels, server_call(): pl.pallas_call(server_kernel, out_shape=[shape((length, width), BF16), sh...  45.2 us
    pallas_call x1, Pallas kernels, grads_call(): pl.pallas_call(grads_kernel, out_shape=[shape((width, columns), BF16), sh...  43.9 us
    pallas_call x1, Pallas kernels, hand_over(): pl.pallas_call(functools.partial(hand_over_kernel, count), out_shape=[jax...  8.26 us

profile of v2, /device:TPU:1, one launch (start us, length us, event | category | flops | bytes accessed | tf_op | source)
XLA Modules:
  0.0 116.7 jit_solution(2561992569581970874)
XLA Ops:
  1.4 1.1 fusion.34
  2.5 0.7 reduce
  3.3 1.4 %convolution_convert_fusion.3 = bf16[128,256]{1,0:T(8,128)(2,1)S(1)} fusion(bf16[1,896,256]{2,1,0:T(8,128)(2,1)} %param.14, bf16[1,1,128,896]{3,2,1,0:T(8,128)(2,1)} %param.11, f32[896]{0:T(1024)S(1)} %reduce, f32[128]{0:T(128)S(1)} %add_rsqrt_fusion), kind=kOutput, calls=%fused_computation.17 | convolution fusion | flops 59211776 | bytes 757760 | tf_op jit(solution)/shard_map/dot_general | solution.py:600
  4.7 0.1 copy.32
  4.8 0.1 copy.31
  5.0 1.7 %bitcast_select_fusion.1.cot_own = bf16[128,896]{1,0:T(8,128)(2,1)} fusion(bf16[1,1,128,896]{3,2,1,0:T(8,128)(2,1)} %param.20, pred[128]{0:T(512)(128)(4,1)S(1)} %iota_compare_fusion.2), kind=kLoop, calls=%fused_computation.51 | loop fusion | flops 114688 | bytes 458880 | tf_op jit(solution)/shard_map/jit(_where)/select_n | solution.py:595
  6.7 1.9 %fusion.9 = bf16[128,896]{1,0:T(8,128)(2,1)S(1)} fusion(bf16[1,896,896]{2,1,0:T(8,128)(2,1)} %param.13, bf16[1,1,128,896]{3,2,1,0:T(8,128)(2,1)S(1)} %copy-done.1, f32[896]{0:T(1024)S(1)} %reduce, f32[128]{0:T(128)S(1)} %add_rsqrt_fusion), kind=kOutput, calls=%fused_computation.12 | convolution fusion | flops 206094336 | bytes 2068480 | tf_op jit(solution)/shard_map/dot_general | solution.py:599
  8.6 0.2 copy.33
  8.8 0.8 fusion.36.normed_own
  9.6 0.3 fusion.31
  10.0 0.2 fusion.40
  10.1 0.6 multiply_divide_fusion
  10.8 0.2 divide_convert_fusion
  11.0 0.2 convolution_convert_fusion.1
  11.2 0.8 copy.35.attended_own
  12.0 1.2 fusion.15.cut_own
  13.2 45.2 %server.1 = (bf16[128,896]{1,0:T(8,128)(2,1)}, bf16[128,896]{1,0:T(8,128)(2,1)}, bf16[8,128,896]{2,1,0:T(8,128)(2,1)}, bf16[8,128,896]{2,1,0:T(8,128)(2,1)}, bf1...) custom-call(bf16[128,896]{1,0:T(8,128)(2,1)} %fusion.15.cut_own, ...), custom_call_target="tpu_custom_call" | custom-call | tf_op jit(solution)/shard_map/server/pallas_call | solution.py:340
  58.4 1.5 %fusion.12 = bf16[128,896]{1,0:T(8,128)(2,1)S(1)} fusion(bf16[128,896]{1,0:T(8,128)(2,1)} %get-tuple-element.30.cut_own, bf16[1,896,896]{2,1,0:T(8,128)(2,1)S(1)} %copy-done), kind=kOutput, calls=%fused_computation.13 | convolution fusion | flops 205635584 | bytes 2064384 | tf_op jit(solution)/shard_map/dot_general | solution.py:609
  60.0 0.2 copy.36
  60.2 0.5 fusion.18
  60.6 0.1 copy.38
  60.7 1.1 fusion.27
  61.9 0.4 fusion.30
  62.4 0.4 fusion.25
  62.8 0.0 copy-done.3
  62.8 0.3 fusion.19
  63.1 0.2 fusion.45
  63.3 0.2 copy.40
  63.5 0.1 copy.39
  63.7 0.7 pad_maximum_fusion.d_own
  64.4 43.9 %grads.1 = (bf16[896,896]{1,0:T(8,128)(2,1)}, bf16[896,256]{1,0:T(8,128)(2,1)}, bf16[896,896]{1,0:T(8,128)(2,1)}, bf16[1216,896]{1,0:T(8,128)(2,1)}, bf16[1216,8...) custom-call(bf16[128,1152]{1,0:T(8,128)(2,1)} %pad_maximum_fusion.d_own, bf16[128,896]{1,0:T(8,128)(2,1)} %get-tuple-element.30.cut_own, ...), custom_call_target="tpu_custom_call" | custom-call | tf_op jit(solution)/shard_map/grads/pallas_call | solution.py:508
  108.3 8.3 %results.1 = (bf16[128,896]{1,0:T(8,128)(2,1)}, bf16[896,896]{1,0:T(8,128)(2,1)}, bf16[896,256]{1,0:T(8,128)(2,1)}, bf16[896,896]{1,0:T(8,128)(2,1)}, bf16[1216,...) custom-call(bf16[128,896]{1,0:T(8,128)(2,1)} %get-tuple-element.29.refs_0_, ...), custom_call_target="tpu_custom_call" | custom-call | tf_op jit(solution)/shard_map/results/pallas_call | solution.py:566
  (15 shorter events, 0.1 us)
Async XLA Ops:
  0.6 11.4 %copy-start = (bf16[1,896,896]{2,1,0:T(8,128)(2,1)S(1)}, bf16[1,896,896]{2,1,0:T(8,128)(2,1)}, u32[]{:S(2)}) copy-start(bf16[1,896,896]{2,1,0:T(8,128)(2,1)} %param.15) | copy-start | bytes 4816900
  0.6 6.1 %copy-start.1 = (bf16[1,1,128,896]{3,2,1,0:T(8,128)(2,1)S(1)}, bf16[1,1,128,896]{3,2,1,0:T(8,128)(2,1)}, u32[]{:S(2)}) copy-start(bf16[1,1,128,896]{3,2,1,0:T(8,128)(2,1)} %param.11) | copy-start | bytes 688132
  8.8 1.3 %copy-start.2 = (bf16[128,896]{0,1:T(8,128)(2,1)}, bf16[128,896]{0,1:T(8,128)(2,1)S(1)}, u32[]{:S(2)}) copy-start(bf16[128,896]{0,1:T(8,128)(2,1)S(1)} %copy.33) | copy-start | bytes 688132
  61.9 0.9 copy-start.3
